TPU v7x, 32 devices: a whole 2x2x4 slice. The times are simulated.
32 devices in a mesh: groups: 2 (over x), seq: 8 (over z, y), dec: 2 (over core).
Axes of the slice: x: 2, y: 2, z: 4, core: 2. Of those that a mesh axis runs over, the one named last changes fastest.
Arguments:
- tokens: bfloat16 [2048, 4096], P(('groups', 'seq')), parts along dimension 0, may hold values from -64 to 64
- norm_gain: float32 [4096], replicated, may hold values from 0.25 to 1.75
- w_query: bfloat16 [4096, 2048], P('seq', 'dec'), may hold values from -0.140625 to 0.140625
- w_key: bfloat16 [4096, 512], P('seq', 'dec'), may hold values from -0.140625 to 0.140625
- w_value: bfloat16 [4096, 512], P('seq', 'dec'), may hold values from -0.09375 to 0.09375
- block_order: int32 [32], P('groups'), parts along dimension 0, may hold values from 0 to 15, as said below
- block_docs: int32 [32], P('groups'), parts along dimension 0, may hold values from 0 to 3, never falling along the last dimension, each value on 1 to 8 neighbouring positions
- head_owner: int32 [8], P('groups'), parts along dimension 0, may hold values from 0 to 3, as said below
- prev_kv: bfloat16 [2048, 2, 4, 128], P(('groups', 'seq', 'dec')), parts along dimension 0, may hold values from -6 to 6
Outputs:
- attended: bfloat16 [2048, 2048], P(('groups', 'seq'), 'dec'), parts along dimension 0
- decode_cache: bfloat16 [2048, 2, 4, 128], P(('groups', 'seq'), None, 'dec'), parts along dimension 0
There are 2 independent parts, one for each index of `groups`. A program takes and returns all parts, laid end to end along the dimension named above; an argument that names none is the same for every part. Nothing has to cross between parts.
Inputs may be any that keep to these rules, and one draw needn't show every extreme that they name: `block_order`: cycle slots 2i and 2i + 1 hold the blocks b and 15 - b for some b; every block stands in exactly one slot. `head_owner`: each key-value head stands in exactly one decode slot.
All inputs are finite; a program needn't handle non-finite values.
Results may differ from a plain program's by a relative error of at most 0.0035.
The roundings to bfloat16 on the way count: a program that leaves them out, or rounds other values in their place, can miss the bound.
Values may be sent and summed in bfloat16 or wider, within the bound.
A program may use at most 64 MiB of HBM per device.

v0:
```python
import math
import jax
import jax.numpy as jnp
from jax import lax
from jax.sharding import PartitionSpec as P

HD = 128


def rotate(values, positions):
    half_width = values.shape[-1] // 2
    frequency = 500000.0 ** (-jnp.arange(half_width, dtype=jnp.float32) / half_width)
    angles = positions[:, None].astype(jnp.float32) * frequency[None, :]
    cosines = jnp.cos(angles)[:, None, :]
    sine_terms = jnp.sin(angles)[:, None, :]
    lower_half = values[..., :half_width]
    upper_half = values[..., half_width:]
    return jnp.concatenate(
        [
            lower_half * cosines - upper_half * sine_terms,
            upper_half * cosines + lower_half * sine_terms,
        ],
        -1,
    )


def per_device(
    tokens, norm_gain, w_query, w_key, w_value, block_order, block_docs, head_owner, prev_kv
):
    rows_dev = tokens.shape[0]
    block_rows = rows_dev // 2
    inputs = tokens.astype(jnp.float32)
    normed = (
        inputs * lax.rsqrt(jnp.mean(inputs * inputs, -1, keepdims=True) + 1e-05) * norm_gain
    ).astype(jnp.bfloat16)

    def add_piece(piece):
        return jnp.dot(normed, piece, preferred_element_type=jnp.float32)

    pieces = (
        lax.all_gather(w_query, "seq", axis=0, tiled=True),
        lax.all_gather(w_key, "seq", axis=0, tiled=True),
        lax.all_gather(w_value, "seq", axis=0, tiled=True),
    )
    query_full, key_full, value_full = tuple((add_piece(piece) for piece in pieces))
    total_rows = rows_dev * lax.axis_size("seq")
    row_ids = jnp.arange(total_rows, dtype=jnp.int32)
    natural = jnp.take(block_order, row_ids // block_rows)
    pos_all = natural * block_rows + row_ids % block_rows
    doc_all = jnp.take(block_docs, natural)
    offset = lax.axis_index("seq") * rows_dev
    my_pos = lax.dynamic_slice_in_dim(pos_all, offset, rows_dev)
    my_doc = lax.dynamic_slice_in_dim(doc_all, offset, rows_dev)
    local_kv = key_full.shape[1] // HD
    local_heads = query_full.shape[1] // HD
    group_size = local_heads // local_kv
    queries = rotate(query_full.reshape(rows_dev, local_heads, HD), my_pos).astype(jnp.bfloat16)
    query_groups = queries.reshape(rows_dev, local_kv, group_size, HD).transpose(1, 2, 0, 3)
    key_rows = (
        rotate(key_full.reshape(rows_dev, local_kv, HD), my_pos)
        .astype(jnp.bfloat16)
        .reshape(rows_dev, local_kv * HD)
    )
    value_rows = value_full.astype(jnp.bfloat16)
    scale = 1.0 / math.sqrt(HD)
    start_max = jnp.full((local_kv, group_size, rows_dev, 1), -jnp.inf, jnp.float32)
    start_sum = jnp.zeros((local_kv, group_size, rows_dev, 1), jnp.float32)
    start_weighted = jnp.zeros((local_kv, group_size, rows_dev, HD), jnp.float32)
    key_piece = lax.all_gather(key_rows, "seq", axis=0, tiled=True)
    value_piece = lax.all_gather(value_rows, "seq", axis=0, tiled=True)
    count = key_piece.shape[0]
    allowed = (pos_all[None, :] <= my_pos[:, None]) & (doc_all[None, :] == my_doc[:, None])

    def update(state):
        running_max, running_sum, weighted = state
        scores = (
            jnp.einsum(
                "ghtd,sgd->ghts",
                query_groups,
                key_piece.reshape(count, local_kv, HD),
                preferred_element_type=jnp.float32,
            )
            * scale
        )
        scores = jnp.where(allowed, scores, -jnp.inf)
        new_max = jnp.max(scores, -1, keepdims=True)
        shift_by = jnp.where(new_max == -jnp.inf, 0.0, new_max)
        weights = jnp.exp(scores - shift_by)
        rescale = jnp.exp(running_max - shift_by)
        running_sum = running_sum * rescale + jnp.sum(weights, -1, keepdims=True)
        weighted = weighted * rescale + jnp.einsum(
            "ghts,sgd->ghtd",
            weights.astype(jnp.bfloat16),
            value_piece.reshape(count, local_kv, HD),
            preferred_element_type=jnp.float32,
        )
        return (new_max, running_sum, weighted)

    final_max, final_sum, final_weighted = lax.cond(
        jnp.any(allowed), update, lambda state: state, (start_max, start_sum, start_weighted)
    )
    attended = (
        (final_weighted / final_sum)
        .transpose(2, 0, 1, 3)
        .reshape(rows_dev, local_heads * HD)
        .astype(jnp.bfloat16)
    )
    head_count = prev_kv.shape[2]
    selector = (head_owner[:, None] == jnp.arange(head_count, dtype=jnp.int32)[None, :]).astype(
        jnp.bfloat16
    )
    ordered = jnp.einsum(
        "tcjd,sj->tcsd", prev_kv, selector, preferred_element_type=jnp.float32
    ).astype(jnp.bfloat16)
    decode_cache = lax.all_to_all(ordered, "dec", split_axis=2, concat_axis=0, tiled=True)
    return (attended, decode_cache)


def solution(mesh):
    in_specs = (
        P(("groups", "seq"), None),
        P(),
        P("seq", "dec"),
        P("seq", "dec"),
        P("seq", "dec"),
        P("groups"),
        P("groups"),
        P("groups"),
        P(("groups", "seq", "dec"), None, None, None),
    )
    out_specs = (P(("groups", "seq"), "dec"), P(("groups", "seq"), None, "dec", None))
    return jax.shard_map(
        per_device, mesh=mesh, in_specs=in_specs, out_specs=out_specs, check_vma=False
    )
```

profile of v0, /device:TPU:0, one launch (start us, length us, event | category | flops | bytes accessed | tf_op | source)
XLA Modules:
  0.0 262.9 jit_solution(15112407311073166945)
XLA Ops:
  8.0 0.7 all-gather.8.cloned.1.call-update
  9.4 1.0 fusion.21
  10.4 0.8 copy.22
  11.2 3.4 %all-to-all-start = ((bf16[64,2,4,128]{3,1,0,2:T(2,128)(2,1)}), bf16[64,2,4,128]{3,1,0,2:T(2,128)(2,1)S(1)}, u32[]{:S(2)}, u32[]{:S(2)}) async-start(bf16[64,2,4,128]{3,1,0,2:T(2,128)(2,1)} %copy.22), calls=%async_computation | async-start | bytes 262144 | tf_op jit(solution)/shard_map/all_to_all | solution.py:115
  14.6 2.0 fusion.58
  16.6 1.9 fusion.59
  18.5 19.9 %select_select_fusion = s32[1024]{0:T(1024)S(1)} fusion(s32[]{:T(128)} %bitcast.35, s32[]{:T(128)} %bitcast.34, s32[]{:T(128)} %bitcast.33, s32[]{:T(128)} %bitcast.32, s32[]{:T(128)} %bitcast.31, s32[]{:T(128)} %bitcast.30, s32[]{:T(128)} %bitcast.29, s32[]{:T(128)} %bitcast.28, s32[]{:T(128)} %bitcast.27, s32[]{:T(128)} %bitcast.26, s32[]{:T(128)} %bitcast.25, ...), kind=kLoop, calls=%fused_computation.72 | loop fusion | flops 83968 | bytes 4224 | tf_op jit(solution)/shard_map/jit(_take)/select_n | solution.py:50
  38.5 10.0 %fusion.29 = s32[1024]{0:T(1024)S(1)} fusion(s32[]{:T(128)} %bitcast.19, s32[]{:T(128)} %bitcast.18, s32[]{:T(128)} %bitcast.17, s32[]{:T(128)} %bitcast.16, s32[]{:T(128)} %bitcast.15, s32[]{:T(128)} %bitcast.14, s32[]{:T(128)} %bitcast.13, s32[]{:T(128)} %bitcast.12, s32[]{:T(128)} %bitcast.11, s32[]{:T(128)} %bitcast.10, s32[]{:T(128)} %bitcast.9, ...), kind=kLoop, calls=%fused_computation.53 | loop fusion | flops 52224 | bytes 4160 | tf_op jit(solution)/shard_map/add | solution.py:49
  48.6 0.8 fusion.57
  50.1 0.9 copy.23
  50.9 1.5 fusion.18
  52.8 9.2 %all-gather.4.cloned.1.call-done = bf16[4096,256]{1,0:T(8,128)(2,1)} async-done(((bf16[512,256]{1,0:T(8,128)(2,1)}), bf16[4096,256]{1,0:T(8,128)(2,1)}) %all-gather.4.cloned.1.call-update) | async-done | bytes 2097168 | tf_op jit(solution)/shard_map/all_gather | solution.py:42
  62.0 2.4 fusion.54
  65.0 32.8 %all_gather.16 = bf16[1024,256]{1,0:T(8,128)(2,1)S(1)} all-gather(bf16[128,256]{1,0:T(8,128)(2,1)S(1)} %bitcast.75), channel_id=1, replica_groups=mesh['groups'=2,'seq'=8,'dec'=2] {'seq'}, dimensions={0}, use_global_device_ids=true | all-gather | bytes 589824 | tf_op jit(solution)/shard_map/all_gather | solution.py:69
  97.8 15.3 %all-gather.8.cloned.1.call-done = bf16[4096,256]{1,0:T(8,128)(2,1)} async-done(((bf16[512,256]{1,0:T(8,128)(2,1)}), bf16[4096,256]{1,0:T(8,128)(2,1)}) %all-gather.8.cloned.1.call-update) | async-done | bytes 2097168 | tf_op jit(solution)/shard_map/all_gather | solution.py:43
  113.1 2.1 convolution_convert_fusion.1
  115.2 33.3 %all_gather.19 = bf16[1024,256]{1,0:T(8,128)(2,1)S(1)} all-gather(bf16[128,256]{1,0:T(8,128)(2,1)S(1)} %convolution_convert_fusion.1), channel_id=1, replica_groups=mesh['groups'=2,'seq'=8,'dec'=2] {'seq'}, dimensions={0}, use_global_device_ids=true | all-gather | bytes 589824 | tf_op jit(solution)/shard_map/all_gather | solution.py:70
  148.5 93.5 %all-gather.6.cloned.1.call-done = bf16[4096,1024]{1,0:T(8,128)(2,1)} async-done(((bf16[512,1024]{1,0:T(8,128)(2,1)}), bf16[4096,1024]{1,0:T(8,128)(2,1)}) %all-gather.6.cloned.1.call-update) | async-done | bytes 8388624 | tf_op jit(solution)/shard_map/all_gather | solution.py:41
  242.0 4.7 %convolution_bitcast_fusion = f32[16,8,8,128]{3,1,2,0:T(8,128)S(1)} fusion(bf16[4096,1024]{1,0:T(8,128)(2,1)} %all-gather.6.cloned.1.call-done, bf16[128,4096]{1,0:T(8,128)(2,1)S(1)} %copy-done.2, f32[4096]{0:T(1024)S(1)} %copy-done.3, f32[128]{0:T(128)S(1)} %add_rsqrt_fusion), kind=kOutput, calls=%fused_computation.25 | convolution fusion | flops 1075838976 | bytes 9978368 | tf_op jit(solution)/shard_map/dot_general | solution.py:38
  247.3 7.8 %conditional.1 = (f32[2,4,128,1]{2,1,0,3:T(4,128)S(1)}, f32[2,4,128,128]{3,2,1,0:T(8,128)S(1)}) conditional(s32[]{:T(128)} %convert_element_type.43, () %tuple.17, (pred[128,1024]{1,0:T(8,128)(4,1)S(1)}, bf16[1024,256]{1,0:T(8,128)(2,1)S(1)}, bf16[2,4,128,128]{3,2,1,0:T(8,128)(2,1)S(1)}, bf16[1024,256]{1,0:T(8,128)(2,1)S(1)}) %tuple.18), branch_computations={%region_2.4_spmd, %region_3.7_spmd} | conditional | flops 548543488 | bytes 33730604 | solution.py:99
  247.4 2.8 %fusion = (f32[2,4,128]{2,1,0:T(4,128)S(1)}, f32[2,4,128,1024]{3,2,1,0:T(8,128)}) fusion(pred[128,1024]{1,0:T(8,128)(4,1)S(1)} %get-tuple-element.3, bf16[2,4,128,128]{3,2,1,0:T(8,128)(2,1)S(1)} %get-tuple-element.10, bf16[1024,2,128,1]{2,1,0,3:T(2,128)(2,1)S(1)} %bitcast.69), kind=kOutput, calls=%fused_computation.2 | convolution fusion | flops 271580160 | bytes 5115904 | tf_op jit(solution)/shard_map/cond/branch_1_fun/ghtd,sgd->ghts/dot_general | solution.py:77
  250.4 3.5 %fusion.6 = f32[2,4,128,128]{3,2,1,0:T(8,128)S(1)} fusion(f32[2,4,128,1024]{3,2,1,0:T(8,128)} %get-tuple-element.26, f32[2,4,128]{2,1,0:T(4,128)S(1)} %get-tuple-element.24, pred[128,1024]{1,0:T(8,128)(4,1)S(1)} %get-tuple-element.3, bf16[1024,2,128,1]{2,1,0,3:T(2,128)(2,1)S(1)} %bitcast.72, f32[2,4,128]{2,1,0:T(4,128)S(1)} %get-tuple-element.23), kind=kOutput, calls=%fused_computation.7 | convolution fusion | flops 272760832 | bytes 5382144 | tf_op jit(solution)/shard_map/cond/branch_1_fun/ghts,sgd->ghtd/dot_general | solution.py:91
  253.9 1.1 fusion.2
  255.5 0.9 convert_element_type.51
  (34 shorter events, 3.8 us)
Async XLA Ops:
  7.2 2.2 copy-start
  7.2 54.9 %all-gather.4.cloned.1.call-start = ((), (), s32[]{:S(2)}) async-start(), calls=%async_computation.1 | async-start | bytes 2359296 | tf_op jit(solution)/shard_map/all_gather | solution.py:42
  7.9 105.2 %all-gather.8.cloned.1.call-start = ((), (), s32[]{:S(2)}) async-start(), calls=%async_computation.3 | async-start | bytes 2359296 | tf_op jit(solution)/shard_map/all_gather | solution.py:43
  8.7 233.3 %all-gather.6.cloned.1.call-start = ((), (), s32[]{:S(2)}) async-start(), calls=%async_computation.2 | async-start | bytes 9437184 | tf_op jit(solution)/shard_map/all_gather | solution.py:41
  9.4 103.7 %copy-start.2 = (bf16[128,4096]{1,0:T(8,128)(2,1)S(1)}, bf16[128,4096]{1,0:T(8,128)(2,1)}, u32[]{:S(2)}) copy-start(bf16[128,4096]{1,0:T(8,128)(2,1)} %param.13) | copy-start | bytes 3145732
  9.4 103.7 %copy-start.3 = (f32[4096]{0:T(1024)S(1)}, f32[4096]{0:T(1024)}, u32[]{:S(2)}) copy-start(f32[4096]{0:T(1024)} %param.14) | copy-start | bytes 49156
  11.2 38.8 %all-to-all-start = ((bf16[64,2,4,128]{3,1,0,2:T(2,128)(2,1)}), bf16[64,2,4,128]{3,1,0,2:T(2,128)(2,1)S(1)}, u32[]{:S(2)}, u32[]{:S(2)}) async-start(bf16[64,2,4,128]{3,1,0,2:T(2,128)(2,1)} %copy.22), calls=%async_computation | async-start | bytes 262144 | tf_op jit(solution)/shard_map/all_to_all | solution.py:115
  250.4 3.6 %copy-start.1 = (f32[2,4,128,1024]{3,2,1,0:T(8,128)S(1)}, f32[2,4,128,1024]{3,2,1,0:T(8,128)}, u32[]{:S(2)}) copy-start(f32[2,4,128,1024]{3,2,1,0:T(8,128)} %get-tuple-element.26) | copy-start | bytes 12582916 | tf_op jit(solution)/shard_map/cond
Sparse Core Ops, SparseCore 0:
  10.1 51.8 all-gather.3
  64.2 48.8 all-gather.7
  115.2 126.7 all-gather.5
where the time goes:
time: 264 us; the launch traced here: 263 us
  waiting for transfers between devices  120 us (45%)
  blocking collectives  66.1 us (25%)
  other arithmetic  34.9 us (13%)
  matrix products  16.5 us (6%)
  between operations  14.6 us (6%)
  local copies, waits for them, and re-layouts  7.21 us (3%)
  starting transfers between devices  3.49 us (1%)
    all_gather x1, waiting for transfers between devices, per_device(): lax.all_gather(w_query, 'seq', axis=0, tiled=True)  93.5 us
    all_gather x1, blocking collectives, per_device(): value_piece = lax.all_gather(value_rows, 'seq', axis=0, tiled=True)  33.3 us
    all_gather x1, blocking collectives, per_device(): key_piece = lax.all_gather(key_rows, 'seq', axis=0, tiled=True)  32.8 us
    select_n x1, other arithmetic, per_device(): doc_all = jnp.take(block_docs, natural)  19.9 us
    all_gather x1, waiting for transfers between devices, per_device(): lax.all_gather(w_value, 'seq', axis=0, tiled=True)  15.3 us
    add x1, other arithmetic, per_device(): pos_all = natural * block_rows + row_ids % block_rows  9.98 us
    all_gather x1, waiting for transfers between devices, per_device(): lax.all_gather(w_key, 'seq', axis=0, tiled=True)  9.24 us
    dot_general x3, matrix products, add_piece(): return jnp.dot(normed, piece, preferred_element_type=jnp.float32)  9.16 us
  transfers between devices with their start and end apart: 4, of which 3 were waited for; matrix products, arithmetic and copies ran while one was open for 17% of the time, Pallas kernels for 0%

commit v1 on v0

--- a/solution.py
+++ b/solution.py
@@ -5,6 +5,19 @@
 from jax.sharding import PartitionSpec as P
 
 HD = 128
+
+
+def drive_pages_all(block_here, peer_axis, dim_i):
+    devs = lax.axis_size(peer_axis)
+    history = list(map(lambda no: (no, (no + 1) % devs), range(devs)))
+
+    def guide_grid_in(z1):
+        if len(z1) == devs:
+            return z1
+        return guide_grid_in([lax.ppermute(z1[0], peer_axis, history), *z1])
+
+    found_now = jnp.concatenate(guide_grid_in([block_here]), dim_i)
+    return jnp.roll(found_now, (lax.axis_index(peer_axis) + 1) * block_here.shape[dim_i], dim_i)
 
 
 def rotate(values, positions):
@@ -66,7 +79,7 @@
     start_max = jnp.full((local_kv, group_size, rows_dev, 1), -jnp.inf, jnp.float32)
     start_sum = jnp.zeros((local_kv, group_size, rows_dev, 1), jnp.float32)
     start_weighted = jnp.zeros((local_kv, group_size, rows_dev, HD), jnp.float32)
-    key_piece = lax.all_gather(key_rows, "seq", axis=0, tiled=True)
+    key_piece = drive_pages_all(key_rows, "seq", 0)
     value_piece = lax.all_gather(value_rows, "seq", axis=0, tiled=True)
     count = key_piece.shape[0]
     allowed = (pos_all[None, :] <= my_pos[:, None]) & (doc_all[None, :] == my_doc[:, None])

time: 264 us -> 266 us (level)
  waiting for transfers between devices: 120 us -> 154 us
  blocking collectives: 66.1 us -> 34.9 us
    all_gather x1 -> x0, blocking collectives: 32.8 us -> none  [per_device(): key_piece = lax.all_gather(key_rows, 'seq', axis=0, tiled=True)]
    all_gather x1, waiting for transfers between devices: 9.24 us -> 38.8 us  [per_device(): lax.all_gather(w_key, 'seq', axis=0, tiled=True)]
    ppermute x0 -> x7, waiting for transfers between devices: none -> 26.5 us  [guide_grid_in(): return guide_grid_in([lax.ppermute(z1[0], peer_axis, history), *z1])]
    all_gather x1, waiting for transfers between devices: 15.3 us -> 0.01 us  [per_device(): lax.all_gather(w_value, 'seq', axis=0, tiled=True)]
    all_gather x1, waiting for transfers between devices: 93.5 us -> 86.7 us  [per_device(): lax.all_gather(w_query, 'seq', axis=0, tiled=True)]
  transfers between devices with their start and end apart: 4 -> 11, of which waited for: 3 -> 7; matrix products, arithmetic and copies ran while one was open for 17% -> 16% of each run, Pallas kernels for 0% -> 0%
where the time goes in v1:
time: 266 us; the launch traced here: 265 us
  waiting for transfers between devices  154 us (58%)
  blocking collectives  34.9 us (13%)
  other arithmetic  34.5 us (13%)
  matrix products  15.9 us (6%)
  between operations  14.7 us (6%)
  local copies, waits for them, and re-layouts  6.49 us (2%)
  starting transfers between devices  4.12 us (2%)
    all_gather x1, waiting for transfers between devices, per_device(): lax.all_gather(w_query, 'seq', axis=0, tiled=True)  86.7 us
    all_gather x1, waiting for transfers between devices, per_device(): lax.all_gather(w_key, 'seq', axis=0, tiled=True)  38.8 us
    all_gather x1, blocking collectives, per_device(): value_piece = lax.all_gather(value_rows, 'seq', axis=0, tiled=True)  34.9 us
    ppermute x7, waiting for transfers between devices, guide_grid_in(): return guide_grid_in([lax.ppermute(z1[0], peer_axis, history), *z1])  26.5 us
    select_n x1, other arithmetic, per_device(): doc_all = jnp.take(block_docs, natural)  19.7 us
    add x1, other arithmetic, per_device(): pos_all = natural * block_rows + row_ids % block_rows  9.9 us
    dot_general x3, matrix products, add_piece(): return jnp.dot(normed, piece, preferred_element_type=jnp.float32)  9.18 us
  transfers between devices with their start and end apart: 11, of which 7 were waited for; matrix products, arithmetic and copies ran while one was open for 16% of the time, Pallas kernels for 0%

profile of v1, /device:TPU:0, one launch (start us, length us, event | category | flops | bytes accessed | tf_op | source)
XLA Modules:
  0.0 264.9 jit_solution(7781226547105861549)
XLA Ops:
  9.5 2.0 fusion.56
  11.4 9.9 %fusion.27 = s32[1024]{0:T(1024)S(1)} fusion(s32[]{:T(128)} %bitcast.15, s32[]{:T(128)} %bitcast.14, s32[]{:T(128)} %bitcast.13, s32[]{:T(128)} %bitcast.12, s32[]{:T(128)} %bitcast.11, s32[]{:T(128)} %bitcast.10, s32[]{:T(128)} %bitcast.9, s32[]{:T(128)} %bitcast.8, s32[]{:T(128)} %bitcast.7, s32[]{:T(128)} %bitcast.6, s32[]{:T(128)} %bitcast.5, ...), kind=kLoop, calls=%fused_computation.67 | loop fusion | flops 52224 | bytes 4160 | tf_op jit(solution)/shard_map/add | solution.py:62
  21.4 1.5 fusion.16
  23.3 38.8 %all-gather.4.cloned.1.call-done = bf16[4096,256]{1,0:T(8,128)(2,1)} async-done(((bf16[512,256]{1,0:T(8,128)(2,1)}), bf16[4096,256]{1,0:T(8,128)(2,1)}) %all-gather.4.cloned.1.call-update) | async-done | bytes 2097168 | tf_op jit(solution)/shard_map/all_gather | solution.py:55
  62.0 2.4 fusion.52
  65.8 6.4 %collective-permute-done = bf16[128,256]{0,1:T(8,128)(2,1)S(1)} collective-permute-done((bf16[128,256]{0,1:T(8,128)(2,1)S(1)}, bf16[128,256]{0,1:T(8,128)(2,1)S(1)}, u32[]{:S(2)}, u32[]{:S(2)}) %collective-permute-start) | collective-permute-done | bytes 65568 | tf_op jit(solution)/shard_map/ppermute | solution.py:17
  72.5 0.8 copy.32
  73.2 3.4 %all-to-all-start = ((bf16[64,2,4,128]{3,1,0,2:T(2,128)(2,1)}), bf16[64,2,4,128]{3,1,0,2:T(2,128)(2,1)S(1)}, u32[]{:S(2)}, u32[]{:S(2)}) async-start(bf16[64,2,4,128]{3,1,0,2:T(2,128)(2,1)} %copy.32), calls=%async_computation | async-start | bytes 262144 | tf_op jit(solution)/shard_map/all_to_all | solution.py:128
  76.6 4.1 %collective-permute-done.1 = bf16[128,256]{0,1:T(8,128)(2,1)S(1)} collective-permute-done((bf16[128,256]{0,1:T(8,128)(2,1)S(1)}, bf16[128,256]{0,1:T(8,128)(2,1)S(1)}, u32[]{:S(2)}, u32[]{:S(2)}) %collective-permute-start.1) | collective-permute-done | bytes 65568 | tf_op jit(solution)/shard_map/ppermute | solution.py:17
  81.4 6.3 %collective-permute-done.2 = bf16[128,256]{0,1:T(8,128)(2,1)S(1)} collective-permute-done((bf16[128,256]{0,1:T(8,128)(2,1)S(1)}, bf16[128,256]{0,1:T(8,128)(2,1)S(1)}, u32[]{:S(2)}, u32[]{:S(2)}) %collective-permute-start.2) | collective-permute-done | bytes 65568 | tf_op jit(solution)/shard_map/ppermute | solution.py:17
  87.6 19.7 %select_select_fusion = s32[1024]{0:T(1024)S(1)} fusion(s32[]{:T(128)} %bitcast.31, s32[]{:T(128)} %bitcast.30, s32[]{:T(128)} %bitcast.29, s32[]{:T(128)} %bitcast.28, s32[]{:T(128)} %bitcast.27, s32[]{:T(128)} %bitcast.26, s32[]{:T(128)} %bitcast.25, s32[]{:T(128)} %bitcast.24, s32[]{:T(128)} %bitcast.23, s32[]{:T(128)} %bitcast.22, s32[]{:T(128)} %bitcast.21, ...), kind=kLoop, calls=%fused_computation.86 | loop fusion | flops 83968 | bytes 4224 | tf_op jit(solution)/shard_map/jit(_take)/select_n | solution.py:63
  107.5 1.0 fusion.55
  109.1 0.9 copy.33
  110.0 4.9 %collective-permute-done.4 = bf16[128,256]{0,1:T(8,128)(2,1)S(1)} collective-permute-done((bf16[128,256]{0,1:T(8,128)(2,1)S(1)}, bf16[128,256]{0,1:T(8,128)(2,1)S(1)}, u32[]{:S(2)}, u32[]{:S(2)}) %collective-permute-start.4) | collective-permute-done | bytes 65568 | tf_op jit(solution)/shard_map/ppermute | solution.py:17
  114.9 2.1 convolution_convert_fusion.1
  117.0 4.8 %collective-permute-done.5 = bf16[128,256]{0,1:T(8,128)(2,1)S(1)} collective-permute-done((bf16[128,256]{0,1:T(8,128)(2,1)S(1)}, bf16[128,256]{0,1:T(8,128)(2,1)S(1)}, u32[]{:S(2)}, u32[]{:S(2)}) %collective-permute-start.5) | collective-permute-done | bytes 65568 | tf_op jit(solution)/shard_map/ppermute | solution.py:17
  121.9 34.9 %all_gather.15 = bf16[1024,256]{1,0:T(8,128)(2,1)S(1)} all-gather(bf16[128,256]{1,0:T(8,128)(2,1)S(1)} %convolution_convert_fusion.1), channel_id=1, replica_groups=mesh['groups'=2,'seq'=8,'dec'=2] {'seq'}, dimensions={0}, use_global_device_ids=true | all-gather | bytes 589824 | tf_op jit(solution)/shard_map/all_gather | solution.py:83
  157.2 86.7 %all-gather.6.cloned.1.call-done = bf16[4096,1024]{1,0:T(8,128)(2,1)} async-done(((bf16[512,1024]{1,0:T(8,128)(2,1)}), bf16[4096,1024]{1,0:T(8,128)(2,1)}) %all-gather.6.cloned.1.call-update) | async-done | bytes 8388624 | tf_op jit(solution)/shard_map/all_gather | solution.py:54
  244.0 4.7 %convolution_bitcast_fusion = f32[16,8,8,128]{3,1,2,0:T(8,128)S(1)} fusion(bf16[4096,1024]{1,0:T(8,128)(2,1)} %all-gather.6.cloned.1.call-done, bf16[128,4096]{1,0:T(8,128)(2,1)S(1)} %copy-done.2, f32[4096]{0:T(1024)S(1)} %copy-done.4, f32[128]{0:T(128)S(1)} %add_rsqrt_fusion), kind=kOutput, calls=%fused_computation.24 | convolution fusion | flops 1075838976 | bytes 9978368 | tf_op jit(solution)/shard_map/dot_general | solution.py:51
  249.3 7.8 %conditional.1 = (f32[2,4,128,1]{2,1,0,3:T(4,128)S(1)}, f32[2,4,128,128]{3,2,1,0:T(8,128)S(1)}) conditional(s32[]{:T(128)} %convert_element_type.46, () %tuple.25, (pred[128,1024]{0,1:T(8,128)(4,1)S(1)}, s32[]{:T(128)}, s32[]{:T(128)}, bf16[2048,256]{0,1:T(8,128)(2,1)S(1)}, bf16[2,4,128,128]{3,2,1,0:T(8,128)(2,1)S(1)}, ...), branch_computations={%region_2.4_spmd, %region_3.7_spmd.clone} | conditional | flops 548543488 | bytes 33730764 | solution.py:112
  249.5 2.8 %fusion.2 = (f32[2,4,128]{2,1,0:T(4,128)S(1)}, f32[2,1024,4,128]{3,1,2,0:T(8,128)}) fusion(pred[128,1024]{0,1:T(8,128)(4,1)S(1)} %get-tuple-element.114, bf16[1024,2,128,1]{0,2,3,1:T(8,128)(2,1)S(1)} %bitcast.82, bf16[2,4,128,128]{3,2,1,0:T(8,128)(2,1)S(1)} %get-tuple-element.117), kind=kOutput, calls=%fused_computation.4 | convolution fusion | flops 271580160 | bytes 5115904 | tf_op jit(solution)/shard_map/cond/branch_1_fun/ghtd,sgd->ghts/dot_general | solution.py:90
  252.5 3.7 %fusion.6 = f32[2,4,128,128]{3,2,1,0:T(8,128)S(1)} fusion(f32[2,1024,4,128]{3,1,2,0:T(8,128)} %get-tuple-element.139, f32[2,4,128]{2,1,0:T(4,128)S(1)} %get-tuple-element.137, pred[128,1024]{0,1:T(8,128)(4,1)S(1)} %get-tuple-element.114, bf16[1024,2,128,1]{2,1,0,3:T(2,128)(2,1)S(1)} %bitcast.88, f32[2,4,128]{2,1,0:T(4,128)S(1)} %get-tuple-element.136), kind=kOutput, calls=%fused_computation.7 | convolution fusion | flops 272760832 | bytes 5382144 | tf_op jit(solution)/shard_map/cond/branch_1_fun/ghts,sgd->ghtd/dot_general | solution.py:104
  256.2 0.9 fusion.1
  257.5 0.9 convert_element_type.54
  (67 shorter events, 6.7 us)
Async XLA Ops:
  7.2 65.0 %copy-start = (bf16[64,2,4,128]{3,2,1,0:T(4,128)(2,1)S(1)}, bf16[64,2,4,128]{3,2,1,0:T(4,128)(2,1)}, u32[]{:S(2)}) copy-start(bf16[64,2,4,128]{3,2,1,0:T(4,128)(2,1)} %param.21) | copy-start | bytes 393220
  7.2 65.0 %copy-start.5 = (s32[4]{0:T(128)S(1)}, s32[4]{0:T(128)}, u32[]{:S(2)}) copy-start(s32[4]{0:T(128)} %param.20) | copy-start | bytes 52
  7.2 73.5 %copy-start.3 = (s32[16]{0:T(128)S(1)}, s32[16]{0:T(128)}, u32[]{:S(2)}) copy-start(s32[16]{0:T(128)} %param.19) | copy-start | bytes 196
  7.2 54.8 %all-gather.4.cloned.1.call-start = ((), (), s32[]{:S(2)}) async-start(), calls=%async_computation.1 | async-start | bytes 2359296 | tf_op jit(solution)/shard_map/all_gather | solution.py:55
  7.9 107.0 %all-gather.8.cloned.1.call-start = ((), (), s32[]{:S(2)}) async-start(), calls=%async_computation.3 | async-start | bytes 2359296 | tf_op jit(solution)/shard_map/all_gather | solution.py:56
  8.7 106.2 %copy-start.2 = (bf16[128,4096]{1,0:T(8,128)(2,1)S(1)}, bf16[128,4096]{1,0:T(8,128)(2,1)}, u32[]{:S(2)}) copy-start(bf16[128,4096]{1,0:T(8,128)(2,1)} %param.13) | copy-start | bytes 3145732
  8.7 106.2 %copy-start.4 = (f32[4096]{0:T(1024)S(1)}, f32[4096]{0:T(1024)}, u32[]{:S(2)}) copy-start(f32[4096]{0:T(1024)} %param.14) | copy-start | bytes 49156
  8.7 235.3 %all-gather.6.cloned.1.call-start = ((), (), s32[]{:S(2)}) async-start(), calls=%async_computation.2 | async-start | bytes 9437184 | tf_op jit(solution)/shard_map/all_gather | solution.py:54
  65.2 7.0 %collective-permute-start = (bf16[128,256]{0,1:T(8,128)(2,1)S(1)}, bf16[128,256]{0,1:T(8,128)(2,1)S(1)}, u32[]{:S(2)}, u32[]{:S(2)}) collective-permute-start(bf16[128,256]{0,1:T(8,128)(2,1)S(1)} %bitcast.85), channel_id=1, source_target_pairs={{0,2},{2,4},{4,6},{6,8},{8,10},{10,12},{12,14},{14,0},{1,3},{3,5},... | collective-permute-start | bytes 196616 | tf_op jit(solution)/shard_map/ppermute | solution.py:17
  72.2 8.5 %collective-permute-start.1 = (bf16[128,256]{0,1:T(8,128)(2,1)S(1)}, bf16[128,256]{0,1:T(8,128)(2,1)S(1)}, u32[]{:S(2)}, u32[]{:S(2)}) collective-permute-start(bf16[128,256]{0,1:T(8,128)(2,1)S(1)} %collective-permute-done), channel_id=1, source_target_pairs={{0,2},{2,4},{4,6},{6,8},{8,10},{10,12},{12,14},{14,0},{1,3},{3,5},... | collective-permute-start | bytes 196616 | tf_op jit(solution)/shard_map/ppermute | solution.py:17
  73.2 35.9 %all-to-all-start = ((bf16[64,2,4,128]{3,1,0,2:T(2,128)(2,1)}), bf16[64,2,4,128]{3,1,0,2:T(2,128)(2,1)S(1)}, u32[]{:S(2)}, u32[]{:S(2)}) async-start(bf16[64,2,4,128]{3,1,0,2:T(2,128)(2,1)} %copy.32), calls=%async_computation | async-start | bytes 262144 | tf_op jit(solution)/shard_map/all_to_all | solution.py:128
  80.7 7.0 %collective-permute-start.2 = (bf16[128,256]{0,1:T(8,128)(2,1)S(1)}, bf16[128,256]{0,1:T(8,128)(2,1)S(1)}, u32[]{:S(2)}, u32[]{:S(2)}) collective-permute-start(bf16[128,256]{0,1:T(8,128)(2,1)S(1)} %collective-permute-done.1), channel_id=1, source_target_pairs={{0,2},{2,4},{4,6},{6,8},{8,10},{10,12},{12,14},{14,0},{1,3},{3,5},... | collective-permute-start | bytes 196616 | tf_op jit(solution)/shard_map/ppermute | solution.py:17
  87.6 19.8 %collective-permute-start.3 = (bf16[128,256]{0,1:T(8,128)(2,1)S(1)}, bf16[128,256]{0,1:T(8,128)(2,1)S(1)}, u32[]{:S(2)}, u32[]{:S(2)}) collective-permute-start(bf16[128,256]{0,1:T(8,128)(2,1)S(1)} %collective-permute-done.2), channel_id=1, source_target_pairs={{0,2},{2,4},{4,6},{6,8},{8,10},{10,12},{12,14},{14,0},{1,3},{3,5},... | collective-permute-start | bytes 196616 | tf_op jit(solution)/shard_map/ppermute | solution.py:17
  107.4 7.5 %collective-permute-start.4 = (bf16[128,256]{0,1:T(8,128)(2,1)S(1)}, bf16[128,256]{0,1:T(8,128)(2,1)S(1)}, u32[]{:S(2)}, u32[]{:S(2)}) collective-permute-start(bf16[128,256]{0,1:T(8,128)(2,1)S(1)} %collective-permute-done.3), channel_id=1, source_target_pairs={{0,2},{2,4},{4,6},{6,8},{8,10},{10,12},{12,14},{14,0},{1,3},{3,5},... | collective-permute-start | bytes 196616 | tf_op jit(solution)/shard_map/ppermute | solution.py:17
  114.9 7.0 %collective-permute-start.5 = (bf16[128,256]{0,1:T(8,128)(2,1)S(1)}, bf16[128,256]{0,1:T(8,128)(2,1)S(1)}, u32[]{:S(2)}, u32[]{:S(2)}) collective-permute-start(bf16[128,256]{0,1:T(8,128)(2,1)S(1)} %collective-permute-done.4), channel_id=1, source_target_pairs={{0,2},{2,4},{4,6},{6,8},{8,10},{10,12},{12,14},{14,0},{1,3},{3,5},... | collective-permute-start | bytes 196616 | tf_op jit(solution)/shard_map/ppermute | solution.py:17
  121.9 35.0 %collective-permute-start.6 = (bf16[128,256]{0,1:T(8,128)(2,1)S(1)}, bf16[128,256]{0,1:T(8,128)(2,1)S(1)}, u32[]{:S(2)}, u32[]{:S(2)}) collective-permute-start(bf16[128,256]{0,1:T(8,128)(2,1)S(1)} %collective-permute-done.5), channel_id=1, source_target_pairs={{0,2},{2,4},{4,6},{6,8},{8,10},{10,12},{12,14},{14,0},{1,3},{3,5},... | collective-permute-start | bytes 196616 | tf_op jit(solution)/shard_map/ppermute | solution.py:17
  252.5 3.7 %copy-start.1 = (f32[2,1024,4,128]{3,1,2,0:T(8,128)S(1)}, f32[2,1024,4,128]{3,1,2,0:T(8,128)}, u32[]{:S(2)}) copy-start(f32[2,1024,4,128]{3,1,2,0:T(8,128)} %get-tuple-element.139) | copy-start | bytes 12582916 | tf_op jit(solution)/shard_map/cond
Sparse Core Ops, SparseCore 0:
  10.1 51.8 all-gather.3
  64.2 48.4 all-gather.7
  114.8 129.1 all-gather.5
